TPU v7x, 256 devices: a whole 4x4x8 slice. The times are simulated.
256 devices in a mesh: img: 8 (over y, x_lo), cls: 8 (over z), emb: 4 (over x_hi, core).
Axes of the slice: x: 4 (x_hi: 2, x_lo: 2; x = x_hi * 2 + x_lo), y: 4, z: 8, core: 2. Of those that a mesh axis runs over, the one named last changes fastest.
Arguments:
- regions: bfloat16 [8192, 1024], P('img', 'emb'), may hold values from -8 to 8
- table: bfloat16 [21504, 1024], P('cls', 'emb'), may hold values from -1 to 1
- shift: float32 [8192], P('img'), may hold values from -0.5 to 0.1
- scale: float32 [8192], P('img'), may hold values from 2 to 20
- labels: int32 [8192], P('img'), may hold values from -1 to 21503, as said below
- valid: int32 [16, 21504], P('img', 'cls'), may hold values 0 or 1
Outputs:
- loss: float32 [], replicated
- region_grad: bfloat16 [8192, 1024], P('img', 'emb')
- table_grad: bfloat16 [21504, 1024], P('cls', 'emb')
Inputs may be any that keep to these rules, and one draw needn't show every extreme that they name: `labels`: -1 marks background; the first region of every image is foreground.
All inputs are finite; a program needn't handle non-finite values. No bound on the sum of `valid` on one device may be relied on, other than what follows from the above.
Results may differ from a plain program's by a relative error of at most 0.0034.
Values may be sent and summed in bfloat16 or wider, within the bound.
No kernel may reach another device: no remote copies, remote signals or barrier semaphores. Data moves between devices by JAX's collectives and lax.ppermute only.
A program may use at most 64 MiB of HBM per device.

v0:
```python
import functools
import jax
import jax.numpy as jnp
from jax import lax
from jax.sharding import Mesh
from jax.sharding import PartitionSpec as P

CLASSES = 21504
REG_IMG = 512
EMB = ("emb_0", "emb_1")
IMG = ("img_0", "img_1")
IMG_CLS_EMB = ("img_0", "img_1", "cls", "emb_0", "emb_1")


def over_axes(shard, axes):
    return functools.reduce(lax.psum, axes, shard)


def focal(logit, target):
    prob = jax.nn.sigmoid(logit)
    return -0.25 * target * (1.0 - prob) ** 2 * jax.nn.log_sigmoid(logit) - 0.75 * (
        1.0 - target
    ) * prob**2 * jax.nn.log_sigmoid(-logit)


def shards(regions, table, shift, scale, labels, valid):
    rows = regions.shape[0]
    class_dev = table.shape[0]
    parts = lax.axis_size(EMB)
    quarter = rows // parts
    start = lax.axis_index(EMB) * quarter
    block = regions.astype(jnp.float32)
    squares = lax.psum(jnp.sum(block * block, axis=1), EMB)
    local_count = jnp.sum((labels >= 0).astype(jnp.float32))
    count = lax.psum(local_count, IMG)
    inv = lax.rsqrt(squares + 1e-06)
    unit = block * inv[:, None]
    unit_b = unit.astype(jnp.bfloat16)
    unit_rows = lax.all_to_all(unit_b, EMB, split_axis=0, concat_axis=1, tiled=True)
    cosine = lax.dot_general(
        unit_rows,
        lax.all_gather(table, EMB, axis=1, tiled=True),
        (((1,), (1,)), ((), ())),
        preferred_element_type=jnp.float32,
    )
    shift_q = lax.dynamic_slice_in_dim(shift, start, quarter, 0)
    scale_q = lax.dynamic_slice_in_dim(scale, start, quarter, 0)
    label_q = lax.dynamic_slice_in_dim(labels, start, quarter, 0)
    image_ids = (start + jnp.arange(quarter, dtype=jnp.int32)) // REG_IMG
    onehot = (image_ids[:, None] == jnp.arange(valid.shape[0], dtype=jnp.int32)[None, :]).astype(
        jnp.float32
    )
    mask = jnp.dot(onehot, valid.astype(jnp.float32), preferred_element_type=jnp.float32)
    class_ids = lax.axis_index("cls") * class_dev + jnp.arange(class_dev, dtype=jnp.int32)
    logit = (cosine + shift_q[:, None]) * scale_q[:, None]
    target = (label_q[:, None] == class_ids[None, :]).astype(jnp.float32)
    term, pullback = jax.vjp(lambda value: focal(value, target), logit)
    dlogit = pullback(jnp.ones_like(term))[0]
    total = over_axes(jnp.sum(term * mask), IMG_CLS_EMB)
    factor = rows * lax.axis_size(IMG) / count
    dscore = (dlogit * mask * scale_q[:, None] * factor).astype(jnp.bfloat16)
    piece = lax.all_gather(dscore, EMB, axis=0, tiled=True)
    dunit_piece = jnp.dot(piece, table, preferred_element_type=jnp.float32)
    table_acc = lax.dot_general(
        piece, unit_b, (((0,), (0,)), ((), ())), preferred_element_type=jnp.float32
    )
    dunit = lax.psum(dunit_piece, "cls")
    radial = lax.psum(jnp.sum(unit * dunit, axis=1), EMB)
    region_grad = (inv[:, None] * (dunit - unit * radial[:, None])).astype(jnp.bfloat16)
    table_grad = lax.psum(table_acc, IMG).astype(jnp.bfloat16)
    loss = total / count / CLASSES
    return (loss, region_grad, table_grad)


def solution(mesh):
    torus = Mesh(
        mesh.devices.reshape(4, 2, mesh.shape["cls"], 2, 2),
        ("img_0", "img_1", "cls", "emb_0", "emb_1"),
    )
    return jax.shard_map(
        shards,
        mesh=torus,
        in_specs=(P(IMG, EMB), P("cls", EMB), P(IMG), P(IMG), P(IMG), P(IMG, "cls")),
        out_specs=(P(), P(IMG, EMB), P("cls", EMB)),
        check_vma=False,
    )
```

profile of v0, /device:TPU:1, one launch (start us, length us, event | category | flops | bytes accessed | tf_op | source)
XLA Modules:
  0.0 273.6 jit_solution(13197794882755454692)
XLA Ops:
  7.2 0.0 all-gather.3.cloned.1.call-start
  7.2 0.7 all-gather.3.cloned.1.call-update
  7.9 1.3 fusion.33
  9.2 9.7 %psum.70 = f32[1024]{0:T(1024)S(1)} all-reduce(f32[1024]{0:T(1024)S(1)} %fusion.33), channel_id=1, replica_groups=mesh['img_0'=4,'img_1'=2,'cls'=8,'emb_0'=2,'emb_1'=2] {'emb_0','emb_1'}, use_global_device_ids=true, to_apply=%region_1.0 | all-reduce | flops 1024 | bytes 8192 | tf_op jit(solution)/shard_map/psum | solution.py:33
  18.9 1.2 fusion.28
  20.2 1.0 copy.9
  21.2 5.2 %all-to-all-start = ((bf16[4,256,256]{1,2,0:T(8,128)(2,1)}), bf16[4,256,256]{1,2,0:T(8,128)(2,1)S(1)}, u32[]{:S(2)}, u32[]{:S(2)}) async-start(bf16[4,256,256]{1,2,0:T(8,128)(2,1)} %copy.9), calls=%async_computation | async-start | bytes 1048576 | tf_op jit(solution)/shard_map/all_to_all | solution.py:39
  26.3 0.6 convert_reduce_fusion
  26.9 24.0 %psum.76 = f32[]{:T(128)} all-reduce(f32[]{:T(128)} %convert_reduce_fusion), channel_id=1, replica_groups=mesh['img_0'=4,'img_1'=2,'cls'=8,'emb_0'=2,'emb_1'=2] {'img_0','img_1'}, use_global_device_ids=true, to_apply=%region_9.11 | all-reduce | flops 1 | bytes 8 | tf_op jit(solution)/shard_map/psum | solution.py:35
  51.0 0.1 dynamic_slice.9
  51.0 0.8 dynamic_slice.11
  51.8 0.8 dynamic_slice.10
  53.3 15.6 %all-gather.3.cloned.1.call-done = bf16[2688,1024]{1,0:T(8,128)(2,1)} async-done(((bf16[2688,256]{1,0:T(8,128)(2,1)}), bf16[2688,1024]{1,0:T(8,128)(2,1)}) %all-gather.3.cloned.1.call-update) | async-done | bytes 5505040 | tf_op jit(solution)/shard_map/all_gather | solution.py:42
  68.9 4.5 %fusion = f32[256,2688]{1,0:T(8,128)S(1)} fusion(bf16[256,1024]{0,1:T(8,128)(2,1)S(1)} %bitcast.11, bf16[2688,1024]{1,0:T(8,128)(2,1)} %all-gather.3.cloned.1.call-done, f32[256]{0:T(256)S(1)} %dynamic_slice.11, f32[256]{0:T(256)S(1)} %dynamic_slice.10), kind=kOutput, calls=%fused_computation.7 | convolution fusion | flops 1410662400 | bytes 8783872 | tf_op jit(solution)/shard_map/dot_general | solution.py:40
  73.4 0.0 copy-start.1
  73.4 9.8 %fusion.12 = (bf16[256,2688]{1,0:T(8,128)(2,1)}, f32[]{:T(128)}) fusion(f32[256,2688]{1,0:T(8,128)S(1)} %fusion, f32[]{:T(128)S(6)} %div.31, f32[256]{0:T(256)S(1)} %dynamic_slice.11, s32[2688]{0:T(1024)S(1)} %iota_add_fusion, s32[256]{0:T(256)S(1)} %dynamic_slice.9, s32[2,2688]{1,0:T(2,128)S(1)} %copy-done.3, s32[256]{0:T(256)S(1)} %and_select_fusion), kind=kOutput, calls=%fused_computation.25 | convolution fusion | flops 47486720 | bytes 4164104 | tf_op jit(solution)/shard_map/dot_general | solution.py:53
  83.2 0.0 all-gather.5.cloned.1.call-update
  83.3 0.0 all-reduce.3.cloned.1.call-start
  83.3 9.4 %psum.71 = f32[]{:T(128)} all-reduce(f32[]{:T(128)} %get-tuple-element.12), channel_id=1, replica_groups=mesh['img_0'=4,'img_1'=2,'cls'=8,'emb_0'=2,'emb_1'=2] {'img_0'}, use_global_device_ids=true, to_apply=%region_3.5 | all-reduce | flops 1 | bytes 8 | tf_op jit(solution)/shard_map/psum | solution.py:16
  92.7 4.4 %psum.72 = f32[]{:T(128)} all-reduce(f32[]{:T(128)} %psum.71), channel_id=1, replica_groups=mesh['img_0'=4,'img_1'=2,'cls'=8,'emb_0'=2,'emb_1'=2] {'img_1'}, use_global_device_ids=true, to_apply=%region_4.6 | all-reduce | flops 1 | bytes 8 | tf_op jit(solution)/shard_map/psum | solution.py:16
  97.1 16.2 %psum.73 = f32[]{:T(128)} all-reduce(f32[]{:T(128)} %psum.72), channel_id=1, replica_groups=mesh['img_0'=4,'img_1'=2,'cls'=8,'emb_0'=2,'emb_1'=2] {'cls'}, use_global_device_ids=true, to_apply=%region_5.7 | all-reduce | flops 1 | bytes 8 | tf_op jit(solution)/shard_map/psum | solution.py:16
  113.3 6.5 %psum.74 = f32[]{:T(128)} all-reduce(f32[]{:T(128)} %psum.73), channel_id=1, replica_groups=mesh['img_0'=4,'img_1'=2,'cls'=8,'emb_0'=2,'emb_1'=2] {'emb_0'}, use_global_device_ids=true, to_apply=%region_6.8 | all-reduce | flops 1 | bytes 8 | tf_op jit(solution)/shard_map/psum | solution.py:16
  119.8 9.1 %psum.75 = f32[]{:T(128)} all-reduce(f32[]{:T(128)} %psum.74), channel_id=1, replica_groups=mesh['img_0'=4,'img_1'=2,'cls'=8,'emb_0'=2,'emb_1'=2] {'emb_1'}, use_global_device_ids=true, to_apply=%region_7.9 | all-reduce | flops 1 | bytes 8 | tf_op jit(solution)/shard_map/psum | solution.py:16
  130.2 1.8 all-gather.5.cloned.1.call-done
  132.0 5.2 %fusion.37 = f32[1024,256]{1,0:T(8,128)} fusion(bf16[1024,2688]{1,0:T(8,128)(2,1)} %all-gather.5.cloned.1.call-done, bf16[2688,256]{1,0:T(8,128)(2,1)S(1)} %copy-done.1), kind=kOutput, calls=%fused_computation.63 | convolution fusion | flops 1409286144 | bytes 7929856 | tf_op jit(solution)/shard_map/dot_general | solution.py:63
  137.2 0.0 all-reduce.3.cloned.1.call-update
  137.3 4.2 %fusion.38 = f32[2688,256]{1,0:T(8,128)S(1)} fusion(bf16[1024,2688]{1,0:T(8,128)(2,1)} %all-gather.5.cloned.1.call-done, bf16[1024,256]{1,0:T(8,128)(2,1)S(1)} %fusion.28), kind=kOutput, calls=%fused_computation.64 | convolution fusion | flops 1409286144 | bytes 8781824 | tf_op jit(solution)/shard_map/dot_general | solution.py:64
  141.5 0.0 copy-start
  141.5 111.4 %all-reduce.4 = bf16[2688,256]{1,0:T(8,128)(2,1)} all-reduce(f32[2688,256]{1,0:T(8,128)S(1)} %fusion.38), channel_id=1, replica_groups=mesh['img_0'=4,'img_1'=2,'cls'=8,'emb_0'=2,'emb_1'=2] {'img_0','img_1'}, use_global_device_ids=true, to_apply=%region_13.15 | all-reduce | flops 688128 | bytes 4128768 | tf_op jit(solution)/shard_map/psum | solution.py:70
  253.0 1.6 fusion.29
  254.6 9.0 %psum.78 = f32[1024]{0:T(1024)S(1)} all-reduce(f32[1024]{0:T(1024)S(1)} %fusion.29), channel_id=1, replica_groups=mesh['img_0'=4,'img_1'=2,'cls'=8,'emb_0'=2,'emb_1'=2] {'emb_0','emb_1'}, use_global_device_ids=true, to_apply=%region_12.14 | all-reduce | flops 1024 | bytes 8192 | tf_op jit(solution)/shard_map/psum | solution.py:68
  263.5 2.4 fusion.32
  (12 shorter events, 0.0 us)
Async XLA Ops:
  7.2 19.2 %copy-start.2 = (s32[1024]{0:T(1024)S(1)}, s32[1024]{0:T(1024)}, u32[]{:S(2)}) copy-start(s32[1024]{0:T(1024)} %param.11) | copy-start | bytes 12292
  7.2 61.7 %all-gather.3.cloned.1.call-start = ((), (), s32[]{:S(2)}) async-start(), calls=%async_computation.1 | async-start | bytes 6881280 | tf_op jit(solution)/shard_map/all_gather | solution.py:42
  21.2 32.1 %all-to-all-start = ((bf16[4,256,256]{1,2,0:T(8,128)(2,1)}), bf16[4,256,256]{1,2,0:T(8,128)(2,1)S(1)}, u32[]{:S(2)}, u32[]{:S(2)}) async-start(bf16[4,256,256]{1,2,0:T(8,128)(2,1)} %copy.9), calls=%async_computation | async-start | bytes 1048576 | tf_op jit(solution)/shard_map/all_to_all | solution.py:39
  26.3 105.7 %all-gather.5.cloned.1.call-start = ((), (), s32[]{:S(2)}) async-start(), calls=%async_computation.2 | async-start | bytes 6881280 | tf_op jit(solution)/shard_map/all_gather | solution.py:62
  68.9 4.5 %copy-start.3 = (s32[2,2688]{1,0:T(2,128)S(1)}, s32[2,2688]{1,0:T(2,128)}, u32[]{:S(2)}) copy-start(s32[2,2688]{1,0:T(2,128)} %param.12) | copy-start | bytes 64516
  73.4 58.6 %copy-start.1 = (bf16[2688,256]{1,0:T(8,128)(2,1)S(1)}, bf16[2688,256]{1,0:T(8,128)(2,1)}, u32[]{:S(2)}) copy-start(bf16[2688,256]{1,0:T(8,128)(2,1)} %param.8) | copy-start | bytes 4128772
  83.3 169.7 %all-reduce.3.cloned.1.call-start = ((), (), s32[]{:S(2)}) async-start(), calls=%async_computation.3 | async-start | bytes 2097152 | tf_op jit(solution)/shard_map/psum | solution.py:67
  141.5 111.5 %copy-start = (bf16[1024,256]{1,0:T(8,128)(2,1)S(1)}, bf16[1024,256]{1,0:T(8,128)(2,1)}, u32[]{:S(2)}) copy-start(bf16[1024,256]{1,0:T(8,128)(2,1)} %param.7) | copy-start | bytes 1572868
Sparse Core Ops, SparseCore 0:
  9.8 59.0 all-gather.2
  83.4 48.5 all-gather.4
  137.4 70.8 all-reduce.2
where the time goes:
time: 274 us
  blocking collectives  200 us (73%)
  matrix products  23.8 us (9%)
  waiting for transfers between devices  18.1 us (7%)
  between operations  17 us (6%)
  other arithmetic  7.09 us (3%)
  starting transfers between devices  5.23 us (2%)
    psum x1, blocking collectives, shards(): table_grad = lax.psum(table_acc, IMG).astype(jnp.bfloat16)  111 us
    psum x5, blocking collectives, over_axes(): return functools.reduce(lax.psum, axes, shard)  45.6 us
    psum x1, blocking collectives, shards(): count = lax.psum(local_count, IMG)  24 us
    all_gather x1, waiting for transfers between devices, shards(): lax.all_gather(table, EMB, axis=1, tiled=True)  15.6 us
    dot_general x1, matrix products, shards(): jnp.dot(onehot, valid.astype(jnp.float32), preferred_element_type=jnp.flo...  9.78 us
    psum x1, blocking collectives, shards(): squares = lax.psum(jnp.sum(block * block, axis=1), EMB)  9.73 us
    psum x1, blocking collectives, shards(): radial = lax.psum(jnp.sum(unit * dunit, axis=1), EMB)  8.96 us
  transfers between devices with their start and end apart: 4, of which 2 were waited for; matrix products, arithmetic and copies ran while one was open for 4% of the time, Pallas kernels for 0%

commit v1 on v0

--- a/solution.py
+++ b/solution.py
@@ -4,6 +4,7 @@
 from jax import lax
 from jax.sharding import Mesh
 from jax.sharding import PartitionSpec as P
+from jax.lax import all_gather
 
 CLASSES = 21504
 REG_IMG = 512
@@ -67,7 +68,7 @@
     dunit = lax.psum(dunit_piece, "cls")
     radial = lax.psum(jnp.sum(unit * dunit, axis=1), EMB)
     region_grad = (inv[:, None] * (dunit - unit * radial[:, None])).astype(jnp.bfloat16)
-    table_grad = lax.psum(table_acc, IMG).astype(jnp.bfloat16)
+    table_grad = jnp.sum(all_gather(table_acc, IMG), axis=0).astype(jnp.bfloat16)
     loss = total / count / CLASSES
     return (loss, region_grad, table_grad)
 

time: 274 us -> 657 us (2.40)
  waiting for transfers between devices: 18.1 us -> 499 us
  blocking collectives: 200 us -> 90.2 us
  other arithmetic: 7.09 us -> 16.8 us
    all_gather x0 -> x1, waiting for transfers between devices: none -> 415 us  [shards(): all_gather(table_acc, IMG)]
    psum x1 -> x0, blocking collectives: 111 us -> none  [shards(): table_grad = lax.psum(table_acc, IMG).astype(jnp.bfloat16)]
    all_gather x1, waiting for transfers between devices: 1.81 us -> 48.6 us  [shards(): piece = lax.all_gather(dscore, EMB, axis=0, tiled=True)]
    psum x1, waiting for transfers between devices: 0.01 us -> 19 us  [shards(): dunit = lax.psum(dunit_piece, 'cls')]
    reduce_sum x0 -> x1, other arithmetic: none -> 9.7 us  [shards(): jnp.sum(all_gather(table_acc, IMG), axis=0).astype(jnp.bfloat16)]
  transfers between devices with their start and end apart: 4 -> 5, of which waited for: 2 -> 4; matrix products, arithmetic and copies ran while one was open for 4% -> 2% of each run, Pallas kernels for 0% -> 0%
where the time goes in v1:
time: 657 us; the launch traced here: 656 us
  waiting for transfers between devices  499 us (76%)
  blocking collectives  90.2 us (14%)
  matrix products  25.2 us (4%)
  between operations  17 us (3%)
  other arithmetic  16.8 us (3%)
    all_gather x1, waiting for transfers between devices, shards(): all_gather(table_acc, IMG)  415 us
    all_gather x1, waiting for transfers between devices, shards(): piece = lax.all_gather(dscore, EMB, axis=0, tiled=True)  48.6 us
    psum x5, blocking collectives, over_axes(): return functools.reduce(lax.psum, axes, shard)  44.8 us
    psum x1, blocking collectives, shards(): count = lax.psum(local_count, IMG)  24 us
    psum x1, waiting for transfers between devices, shards(): dunit = lax.psum(dunit_piece, 'cls')  19 us
    all_gather x1, waiting for transfers between devices, shards(): lax.all_gather(table, EMB, axis=1, tiled=True)  15.6 us
  transfers between devices with their start and end apart: 5, of which 4 were waited for; matrix products, arithmetic and copies ran while one was open for 2% of the time, Pallas kernels for 0%

profile of v1, /device:TPU:1, one launch (start us, length us, event | category | flops | bytes accessed | tf_op | source)
XLA Modules:
  0.0 656.2 jit_solution(6289224377994652833)
XLA Ops:
  7.2 0.0 all-gather.5.cloned.1.call-start
  7.2 0.7 all-gather.5.cloned.1.call-update
  7.9 1.3 fusion.33
  9.2 9.7 %psum.63 = f32[1024]{0:T(1024)S(1)} all-reduce(f32[1024]{0:T(1024)S(1)} %fusion.33), channel_id=1, replica_groups=mesh['img_0'=4,'img_1'=2,'cls'=8,'emb_0'=2,'emb_1'=2] {'emb_0','emb_1'}, use_global_device_ids=true, to_apply=%region_1.0 | all-reduce | flops 1024 | bytes 8192 | tf_op jit(solution)/shard_map/psum | solution.py:34
  18.9 1.2 fusion.28
  20.2 1.0 copy.9
  21.2 5.2 all-to-all-start
  26.3 0.6 convert_reduce_fusion
  26.9 24.0 %psum.69 = f32[]{:T(128)} all-reduce(f32[]{:T(128)} %convert_reduce_fusion), channel_id=1, replica_groups=mesh['img_0'=4,'img_1'=2,'cls'=8,'emb_0'=2,'emb_1'=2] {'img_0','img_1'}, use_global_device_ids=true, to_apply=%region_9.11 | all-reduce | flops 1 | bytes 8 | tf_op jit(solution)/shard_map/psum | solution.py:36
  51.0 0.1 dynamic_slice.9
  51.0 0.8 dynamic_slice.11
  51.8 0.8 dynamic_slice.10
  53.3 15.6 %all-gather.5.cloned.1.call-done = bf16[2688,1024]{1,0:T(8,128)(2,1)} async-done(((bf16[2688,256]{1,0:T(8,128)(2,1)}), bf16[2688,1024]{1,0:T(8,128)(2,1)}) %all-gather.5.cloned.1.call-update) | async-done | bytes 5505040 | tf_op jit(solution)/shard_map/all_gather | solution.py:43
  68.9 4.5 fusion
  73.4 9.8 %fusion.12 = (bf16[256,2688]{1,0:T(8,128)(2,1)}, f32[]{:T(128)}) fusion(f32[256,2688]{1,0:T(8,128)S(1)} %fusion, f32[]{:T(128)S(6)} %div.31, f32[256]{0:T(256)S(1)} %dynamic_slice.11, s32[2688]{0:T(1024)S(1)} %iota_add_fusion, s32[256]{0:T(256)S(1)} %dynamic_slice.9, s32[2,2688]{1,0:T(2,128)S(1)} %copy-done.3, s32[256]{0:T(256)S(1)} %and_select_fusion), kind=kOutput, calls=%fused_computation.25 | convolution fusion | flops 47486720 | bytes 4164104 | tf_op jit(solution)/shard_map/dot_general | solution.py:54
  83.2 0.0 all-gather.7.cloned.1.call-update
  83.3 0.0 all-reduce.2.cloned.1.call-start
  83.3 48.6 %all-gather.7.cloned.1.call-done = bf16[1024,2688]{1,0:T(8,128)(2,1)} async-done(((bf16[256,2688]{1,0:T(8,128)(2,1)}), bf16[1024,2688]{1,0:T(8,128)(2,1)}) %all-gather.7.cloned.1.call-update) | async-done | bytes 5505040 | tf_op jit(solution)/shard_map/all_gather | solution.py:63
  131.9 5.2 fusion.37
  137.1 0.0 all-gather.9.cloned.1.call-start
  137.2 5.7 fusion.38
  142.9 9.5 %psum.64 = f32[]{:T(128)} all-reduce(f32[]{:T(128)} %get-tuple-element.12), channel_id=1, replica_groups=mesh['img_0'=4,'img_1'=2,'cls'=8,'emb_0'=2,'emb_1'=2] {'img_0'}, use_global_device_ids=true, to_apply=%region_3.5 | all-reduce | flops 1 | bytes 8 | tf_op jit(solution)/shard_map/psum | solution.py:17
  152.4 4.4 psum.65
  156.8 15.6 %psum.66 = f32[]{:T(128)} all-reduce(f32[]{:T(128)} %psum.65), channel_id=1, replica_groups=mesh['img_0'=4,'img_1'=2,'cls'=8,'emb_0'=2,'emb_1'=2] {'cls'}, use_global_device_ids=true, to_apply=%region_5.7 | all-reduce | flops 1 | bytes 8 | tf_op jit(solution)/shard_map/psum | solution.py:17
  172.4 5.9 psum.67
  178.3 9.4 %psum.68 = f32[]{:T(128)} all-reduce(f32[]{:T(128)} %psum.67), channel_id=1, replica_groups=mesh['img_0'=4,'img_1'=2,'cls'=8,'emb_0'=2,'emb_1'=2] {'emb_1'}, use_global_device_ids=true, to_apply=%region_7.9 | all-reduce | flops 1 | bytes 8 | tf_op jit(solution)/shard_map/psum | solution.py:17
  189.1 19.0 %all-reduce.2.cloned.1.call-done = f32[1024,256]{1,0:T(8,128)} async-done(((f32[1024,256]{1,0:T(8,128)}), f32[1024,256]{1,0:T(8,128)}) %all-reduce.2.cloned.1.call-update) | async-done | bytes 1048592 | tf_op jit(solution)/shard_map/psum | solution.py:68
  208.0 1.6 fusion.29
  209.6 11.7 %psum.71 = f32[1024]{0:T(1024)S(1)} all-reduce(f32[1024]{0:T(1024)S(1)} %fusion.29), channel_id=1, replica_groups=mesh['img_0'=4,'img_1'=2,'cls'=8,'emb_0'=2,'emb_1'=2] {'emb_0','emb_1'}, use_global_device_ids=true, to_apply=%region_12.14 | all-reduce | flops 1024 | bytes 8192 | tf_op jit(solution)/shard_map/psum | solution.py:69
  221.3 2.4 fusion.32
  223.7 415.1 %all-gather.9.cloned.1.call-done = f32[21504,256]{1,0:T(8,128)} async-done(((f32[2688,256]{1,0:T(8,128)}), f32[21504,256]{1,0:T(8,128)}) %all-gather.9.cloned.1.call-update) | async-done | bytes 22020112 | tf_op jit(solution)/shard_map/all_gather | solution.py:71
  638.8 9.7 %reduce_sum.49 = bf16[2688,256]{1,0:T(8,128)(2,1)} reduce(f32[8,2688,256]{2,1,0:T(8,128)} %bitcast.11, f32[]{:T(128)} %constant.52.clone.1), dimensions={0}, to_apply=%region_13.15 | reduce | flops 4816896 | bytes 23396356 | tf_op jit(solution)/shard_map/reduce_sum | solution.py:71
  (15 shorter events, 0.1 us)
Async XLA Ops:
  7.2 19.2 %copy-start.2 = (s32[1024]{0:T(1024)S(1)}, s32[1024]{0:T(1024)}, u32[]{:S(2)}) copy-start(s32[1024]{0:T(1024)} %param.11) | copy-start | bytes 12292
  7.2 61.7 %all-gather.5.cloned.1.call-start = ((), (), s32[]{:S(2)}) async-start(), calls=%async_computation.1 | async-start | bytes 6881280 | tf_op jit(solution)/shard_map/all_gather | solution.py:43
  21.2 32.1 %all-to-all-start = ((bf16[4,256,256]{1,2,0:T(8,128)(2,1)}), bf16[4,256,256]{1,2,0:T(8,128)(2,1)S(1)}, u32[]{:S(2)}, u32[]{:S(2)}) async-start(bf16[4,256,256]{1,2,0:T(8,128)(2,1)} %copy.9), calls=%async_computation | async-start | bytes 1048576 | tf_op jit(solution)/shard_map/all_to_all | solution.py:40
  26.3 105.6 %all-gather.7.cloned.1.call-start = ((), (), s32[]{:S(2)}) async-start(), calls=%async_computation.2 | async-start | bytes 6881280 | tf_op jit(solution)/shard_map/all_gather | solution.py:63
  68.9 4.5 copy-start.3
  73.4 58.5 %copy-start.1 = (bf16[2688,256]{1,0:T(8,128)(2,1)S(1)}, bf16[2688,256]{1,0:T(8,128)(2,1)}, u32[]{:S(2)}) copy-start(bf16[2688,256]{1,0:T(8,128)(2,1)} %param.8) | copy-start | bytes 4128772
  83.3 124.8 %all-reduce.2.cloned.1.call-start = ((), (), s32[]{:S(2)}) async-start(), calls=%async_computation.3 | async-start | bytes 2097152 | tf_op jit(solution)/shard_map/psum | solution.py:68
  137.1 501.7 %all-gather.9.cloned.1.call-start = ((), (), s32[]{:S(2)}) async-start(), calls=%async_computation.4 | async-start | bytes 24772608 | tf_op jit(solution)/shard_map/all_gather | solution.py:71
  142.9 65.1 %copy-start = (bf16[1024,256]{1,0:T(8,128)(2,1)S(1)}, bf16[1024,256]{1,0:T(8,128)(2,1)}, u32[]{:S(2)}) copy-start(bf16[1024,256]{1,0:T(8,128)(2,1)} %param.7) | copy-start | bytes 1572868
Sparse Core Ops, SparseCore 0:
  9.8 59.0 all-gather.4
  83.4 48.5 all-gather.6
  137.3 70.7 all-reduce.1
  209.7 429.1 all-gather.8
